TPU v7x, 512 devices: a 4x2x32 block of a 4x8x32 slice. The times are simulated.
512 devices in a mesh: parts: 2 (over y), seq: 32 (over z), head: 8 (over x, core).
Axes of the slice: x: 4, y: 2, z: 32, core: 2. Of those that a mesh axis runs over, the one named last changes fastest.
The devices are a block of a 4x8x32 slice.
Arguments:
- hidden: bfloat16 [48, 12288], P(('parts', 'head'), 'seq'), parts along dimension 0, may hold values from -600 to 600
- norm_gain: float32 [12288], P('seq'), may hold values from 0.1 to 1.9
- w_query: bfloat16 [12288, 12288], P('seq', 'head'), may hold values from -0.0546875 to 0.0546875
- w_key: bfloat16 [12288, 1024], P('seq', 'head'), may hold values from -0.0546875 to 0.0546875
- w_value: bfloat16 [12288, 1024], P('seq', 'head'), may hold values from -0.0546875 to 0.0546875
- w_out: bfloat16 [12288, 12288], P('head', 'seq'), may hold values from -0.0546875 to 0.0546875
- lengths: int32 [48], P('parts'), parts along dimension 0, may hold values from 1 to 4096, as said below
- key_cache: bfloat16 [48, 8, 4096, 128], P('parts', 'head', 'seq'), parts along dimension 0, may hold values from -600 to 600, as said below
- value_cache: bfloat16 [48, 8, 4096, 128], P('parts', 'head', 'seq'), parts along dimension 0, may hold values from -6 to 6
Outputs:
- attn_out: bfloat16 [48, 12288], P(('parts', 'head'), 'seq'), parts along dimension 0
There are 2 independent parts, one for each index of `parts`. A program takes and returns all parts, laid end to end along the dimension named above; an argument that names none is the same for every part. Nothing has to cross between parts.
Inputs may be any that keep to these rules, and one draw needn't show every extreme that they name: Sequence b holds lengths[b] cached tokens at positions 0 to lengths[b] - 1; its new token takes position lengths[b]. `key_cache`: positions at or past a sequence's length hold no data.
All inputs are finite; a program needn't handle non-finite values.
Results may differ from a plain program's by a relative error of at most 0.0075.
The roundings to bfloat16 on the way count: a program that leaves them out, or rounds other values in their place, can miss the bound.
Values may be sent and summed in bfloat16 or wider, within the bound.
No kernel may reach another device: no remote copies, remote signals or barrier semaphores. Data moves between devices by JAX's collectives and lax.ppermute only.
A program may use at most 64 MiB of HBM per device.

v0:
```python
import math
import jax
import jax.numpy as jnp
from jax import lax
from jax.sharding import PartitionSpec as P

D = 12288
EPSILON = 1e-05


def in_order(tiles, dim):
    tiles = jnp.moveaxis(tiles, 0, dim)
    dims = tiles.shape
    return tiles.reshape(*dims[:dim], dims[dim] * dims[dim + 1], *dims[dim + 2 :])


def sent_to_all(x, axis):
    copies = jnp.broadcast_to(x, (lax.axis_size(axis), *x.shape))
    return lax.all_to_all(copies, axis, split_axis=0, concat_axis=0, tiled=True)


def gather_directly(x, axis, dim):
    return in_order(sent_to_all(x, axis), dim)


def cut_along(x, dim, peers):
    before, after = (x.shape[:dim], x.shape[dim + 1 :])
    return jnp.moveaxis(x.reshape(*before, peers, -1, *after), dim, 0)


def summed_on_arrival(x, axis, dim):
    tiles = cut_along(x, dim, lax.axis_size(axis))
    arrived = lax.all_to_all(tiles, axis, split_axis=0, concat_axis=0, tiled=True)
    return arrived.sum(axis=0)


def in_one_piece(arrays, axis, dim, along):
    ends, at = ([], 0)
    for a in arrays[:-1]:
        at += a.shape[along]
        ends.append(at)
    both = jnp.concatenate(arrays, axis=along)
    return tuple(jnp.split(summed_on_arrival(both, axis, dim), ends, axis=along))


def in_one_piece_2(arrays, axis, dim, along):
    ends, at = ([], 0)
    for a in arrays[:-1]:
        at += a.shape[along]
        ends.append(at)
    both = jnp.concatenate(arrays, axis=along)
    return tuple(jnp.split(lax.all_gather(both, axis, axis=dim, tiled=True), ends, axis=along))


def side_by_side(arrays, axis, dim, along):
    widths = [math.prod(a.shape[along:]) for a in arrays]
    both = jnp.concatenate(
        [a.reshape(*a.shape[:along], w) for a, w in zip(arrays, widths)], axis=along
    )
    result = lax.all_gather(both, axis, axis=dim, tiled=True)
    tiles = jnp.split(result, [sum(widths[:k]) for k in range(1, len(widths))], axis=along)
    return tuple(
        (b.reshape(*result.shape[:along], *a.shape[along:]) for a, b in zip(arrays, tiles))
    )


def fold_blocks(totals, pieces):
    new_max = jnp.maximum(totals[0], jnp.max(pieces[0], axis=0))
    piece_factor = jnp.exp(pieces[0] - new_max[None])
    den_total = jnp.sum(piece_factor * pieces[1], axis=0)
    acc_total = jnp.sum(piece_factor[..., None] * pieces[2], axis=0)
    return (new_max, den_total, acc_total)


def local(hidden, norm_gain, w_query, w_key, w_value, w_out, lengths, key_cache, value_cache):
    batch_size, kv_local, block_len, head_size = key_cache.shape
    group_size = w_query.shape[1] // (kv_local * head_size)
    token_rows = gather_directly(hidden, "head", 0)
    widened = token_rows.astype(jnp.float32)
    square_local = jnp.sum(widened * widened, axis=1)
    scaled = (widened * norm_gain).astype(jnp.bfloat16)
    query_part = jnp.dot(scaled, w_query, preferred_element_type=jnp.float32)
    key_part = jnp.dot(scaled, w_key, preferred_element_type=jnp.float32)
    value_part = jnp.dot(scaled, w_value, preferred_element_type=jnp.float32)
    query_factor = float(head_size) ** (-0.5)
    square_tiled = jnp.broadcast_to(square_local[:, None], (batch_size, lax.axis_size("seq")))
    query_sum, key_sum, value_sum, norm_column = (
        summed_on_arrival(query_part, "seq", 1),
        *in_one_piece((key_part, value_part), "seq", 1, 0),
        summed_on_arrival(square_tiled, "seq", 1),
    )
    norm_total = norm_column[:, 0]
    inverse_rms = lax.rsqrt(norm_total / D + EPSILON)[:, None]
    queries = (query_sum * inverse_rms * query_factor).astype(jnp.bfloat16)
    new_keys = (key_sum * inverse_rms).astype(jnp.bfloat16)
    new_values = (value_sum * inverse_rms).astype(jnp.bfloat16)
    queries, new_keys, new_values = (
        lax.all_gather(queries, "seq", axis=1, tiled=True),
        *in_one_piece_2((new_keys, new_values), "seq", 1, 0),
    )
    grouped = queries.reshape(batch_size, kv_local, group_size, head_size)
    scores = jnp.einsum("bkgd,bkpd->bkgp", grouped, key_cache, preferred_element_type=jnp.float32)
    offset = lax.axis_index("seq") * block_len
    positions = offset + jnp.arange(block_len, dtype=jnp.int32)
    live_mask = (positions[None, :] < lengths[:, None])[:, None, None, :]
    block_max = jnp.max(jnp.where(live_mask, scores, -1e30), axis=-1)
    shifted = jnp.where(live_mask, scores - block_max[..., None], 0.0)
    weights = jnp.where(live_mask, jnp.exp(shifted), 0.0).astype(jnp.bfloat16)
    block_den = jnp.sum(weights.astype(jnp.float32), axis=-1)
    block_acc = jnp.einsum(
        "bkgp,bkpd->bkgd", weights, value_cache, preferred_element_type=jnp.float32
    )
    self_score = jnp.einsum(
        "oips,ois->oip",
        grouped,
        new_keys.reshape(batch_size, kv_local, head_size),
        preferred_element_type=jnp.float32,
    )
    initial = (
        jnp.full(block_max.shape, -1e30, jnp.float32),
        jnp.zeros(block_den.shape, jnp.float32),
        jnp.zeros(block_acc.shape, jnp.float32),
    )
    global_max, den_merged, acc_merged = fold_blocks(
        initial, side_by_side((block_max[None], block_den[None], block_acc[None]), "seq", 0, 4)
    )
    top_score = jnp.maximum(global_max, self_score)
    factors = jnp.exp(global_max - top_score)
    den_sum = den_merged * factors
    acc_sum = acc_merged * factors[..., None]
    own_weight = jnp.exp(self_score - top_score)
    denominator = den_sum + own_weight
    numerator = acc_sum + own_weight[..., None] * new_values.reshape(
        batch_size, kv_local, 1, head_size
    ).astype(jnp.float32)
    mixed = (
        (numerator / denominator[..., None])
        .astype(jnp.bfloat16)
        .reshape(batch_size, kv_local * group_size * head_size)
    )
    output = summed_on_arrival(jnp.dot(mixed, w_out, preferred_element_type=jnp.float32), "head", 0)
    return output.astype(jnp.bfloat16)


def solution(mesh):
    return jax.shard_map(
        local,
        mesh=mesh,
        in_specs=(
            P(("parts", "head"), "seq"),
            P("seq"),
            P("seq", "head"),
            P("seq", "head"),
            P("seq", "head"),
            P("head", "seq"),
            P("parts"),
            P("parts", "head", "seq", None),
            P("parts", "head", "seq", None),
        ),
        out_specs=P(("parts", "head"), "seq"),
        check_vma=False,
    )
```

profile of v0, /device:TPU:33, one launch (start us, length us, event | category | flops | bytes accessed | tf_op | source)
XLA Modules:
  0.0 357.4 jit_solution(9531133762320092091)
XLA Ops:
  6.6 1.4 broadcast_in_dim.49
  8.0 44.7 %all-to-all-start = ((bf16[8,3,384]{2,1,0:T(4,128)(2,1)}), bf16[8,3,384]{2,1,0:T(4,128)(2,1)S(1)}, u32[]{:S(2)}, u32[]{:S(2)}) async-start(bf16[8,3,384]{2,1,0:T(4,128)(2,1)} %broadcast_in_dim.49), calls=%async_computation | async-start | bytes 49152 | tf_op jit(solution)/shard_map/all_to_all | solution.py:19
  52.7 1.7 copy.66
  54.4 3.0 all-to-all-done
  57.4 0.8 multiply_reduce_fusion
  58.9 6.8 %all-to-all-start.2 = ((f32[32,24,1]{1,2,0:T(1,128)}), f32[32,24,1]{1,2,0:T(1,128)S(1)}, u32[]{:S(2)}, u32[]{:S(2)}) async-start(f32[32,24,1]{1,2,0:T(1,128)} %transpose.24), calls=%async_computation.2 | async-start | bytes 32768 | tf_op jit(solution)/shard_map/all_to_all | solution.py:33
  66.3 1.6 convolution_bitcast_fusion
  67.8 1.1 reshape.206
  68.9 17.3 %all-to-all-done.2 = f32[32,24,1]{1,2,0:T(1,128)S(1)} async-done(((f32[32,24,1]{1,2,0:T(1,128)}), f32[32,24,1]{1,2,0:T(1,128)S(1)}, u32[]{:S(2)}, u32[]{:S(2)}) %all-to-all-start.2) | async-done | bytes 3104 | tf_op jit(solution)/shard_map/all_to_all | solution.py:33
  86.2 4.8 %all-to-all-start.1 = ((f32[32,1,1152]{2,1,0:T(1,128)}), f32[32,1,1152]{2,1,0:T(1,128)S(1)}, u32[]{:S(2)}, u32[]{:S(2)}) async-start(f32[32,1,1152]{2,1,0:T(1,128)} %reshape.206), calls=%async_computation.1 | async-start | bytes 294912 | tf_op jit(solution)/shard_map/all_to_all | solution.py:33
  91.9 27.9 %all-to-all-done.1 = f32[32,1,1152]{2,1,0:T(1,128)S(1)} async-done(((f32[32,1,1152]{2,1,0:T(1,128)}), f32[32,1,1152]{2,1,0:T(1,128)S(1)}, u32[]{:S(2)}, u32[]{:S(2)}) %all-to-all-start.1) | async-done | bytes 147488 | tf_op jit(solution)/shard_map/all_to_all | solution.py:33
  120.3 1.0 reduce.10
  121.7 38.6 %all-gather = bf16[32,48,24]{1,2,0:T(8,128)(2,1)S(1)} all-gather(bf16[1,48,24]{1,2,0:T(8,128)(2,1)S(1)} %fusion.13), channel_id=1, replica_groups=mesh['parts'=2,'seq'=32,'head'=8] {'seq'}, dimensions={0}, use_global_device_ids=true | all-gather | bytes 76032 | tf_op jit(solution)/shard_map/all_gather | solution.py:98
  162.7 0.9 copy.72
  163.6 1.0 fusion.14
  164.7 1.0 fusion.15
  166.0 30.1 %all_to_all.25 = f32[32,1,192]{2,1,0:T(1,128)S(1)} all-to-all(f32[32,1,192]{2,1,0:T(1,128)S(1)} %reshape.208), channel_id=1, replica_groups=mesh['parts'=2,'seq'=32,'head'=8] {'seq'}, dimensions={0} | all-to-all | bytes 49152 | tf_op jit(solution)/shard_map/all_to_all | solution.py:33
  197.1 42.9 %all-gather.1 = bf16[32,4,48]{2,1,0:T(4,128)(2,1)S(1)} all-gather(bf16[1,4,48]{2,1,0:T(4,128)(2,1)S(1)} %maximum_bitcast_fusion), channel_id=1, replica_groups=mesh['parts'=2,'seq'=32,'head'=8] {'seq'}, dimensions={0}, use_global_device_ids=true | all-gather | bytes 12672 | tf_op jit(solution)/shard_map/all_gather | solution.py:52
  240.4 61.3 %all-gather.4.cloned.1.call-done = f32[32,24,1,12,130]{4,1,3,2,0:T(8,128)} async-done(((f32[1,24,1,12,130]{4,1,3,2,0:T(8,128)}), f32[32,24,1,12,130]{4,1,3,2,0:T(8,128)}) %all-gather.4.cloned.1.call-update) | async-done | bytes 4792336 | tf_op jit(solution)/shard_map/all_gather | solution.py:60
  301.7 9.1 %fusion.18 = (f32[32,24,1,12,1]{4,1,3,2,0:T(8,128)}, f32[24,12]{0,1:T(8,128)S(1)}, f32[32,24,1,12,1]{4,1,3,2,0:T(8,128)}) fusion(f32[32,24,1,12,130]{4,1,3,2,0:T(8,128)} %all-gather.4.cloned.1.call-done), kind=kLoop, calls=%fused_computation.45 | loop fusion | flops 8928 | bytes 148608 | tf_op jit(solution)/shard_map/split | solution.py:61
  310.8 3.5 copy.88
  314.3 3.5 copy.87
  318.4 5.1 %fusion = f32[24,12,128]{2,0,1:T(8,128)S(1)} fusion(f32[32,24,1,12,130]{4,1,3,2,0:T(8,128)} %all-gather.4.cloned.1.call-done, f32[32,24,12]{1,2,0:T(8,128)S(1)} %copy.74), kind=kLoop, calls=%fused_computation.1 | loop fusion | flops 2322432 | bytes 4902912 | tf_op jit(solution)/shard_map/reduce_sum | solution.py:71
  324.0 25.8 %all_to_all.26 = f32[8,3,384]{2,1,0:T(4,128)S(1)} all-to-all(f32[8,3,384]{2,1,0:T(4,128)S(1)} %copy.80), channel_id=1, replica_groups=mesh['parts'=2,'seq'=32,'head'=8] {'head'}, dimensions={0} | all-to-all | bytes 73728 | tf_op jit(solution)/shard_map/all_to_all | solution.py:33
  (56 shorter events, 8.7 us)
Async XLA Ops:
  6.5 317.2 %copy-start = (bf16[1536,384]{1,0:T(8,128)(2,1)S(1)}, bf16[1536,384]{1,0:T(8,128)(2,1)}, u32[]{:S(2)}) copy-start(bf16[1536,384]{1,0:T(8,128)(2,1)} %param.14) | copy-start | bytes 3538948
  6.6 154.1 %copy-start.1 = (bf16[24,1,128,128]{3,2,1,0:T(8,128)(2,1)S(1)}, bf16[24,1,128,128]{3,2,1,0:T(8,128)(2,1)}, u32[]{:S(2)}) copy-start(bf16[24,1,128,128]{3,2,1,0:T(8,128)(2,1)} %param.16) | copy-start | bytes 2359300
  8.0 49.4 %all-to-all-start = ((bf16[8,3,384]{2,1,0:T(4,128)(2,1)}), bf16[8,3,384]{2,1,0:T(4,128)(2,1)S(1)}, u32[]{:S(2)}, u32[]{:S(2)}) async-start(bf16[8,3,384]{2,1,0:T(4,128)(2,1)} %broadcast_in_dim.49), calls=%async_computation | async-start | bytes 49152 | tf_op jit(solution)/shard_map/all_to_all | solution.py:19
  57.4 8.9 %copy-start.3 = (bf16[8,3,384]{2,1,0:T(4,128)(2,1)}, bf16[8,3,384]{2,1,0:T(4,128)(2,1)S(1)}, u32[]{:S(2)}) copy-start(bf16[8,3,384]{2,1,0:T(4,128)(2,1)S(1)} %all-to-all-done) | copy-start | bytes 55300
  58.9 27.3 %all-to-all-start.2 = ((f32[32,24,1]{1,2,0:T(1,128)}), f32[32,24,1]{1,2,0:T(1,128)S(1)}, u32[]{:S(2)}, u32[]{:S(2)}) async-start(f32[32,24,1]{1,2,0:T(1,128)} %transpose.24), calls=%async_computation.2 | async-start | bytes 32768 | tf_op jit(solution)/shard_map/all_to_all | solution.py:33
  67.8 93.6 %copy-start.2 = (bf16[24,1,128,128]{3,2,1,0:T(8,128)(2,1)S(1)}, bf16[24,1,128,128]{3,2,1,0:T(8,128)(2,1)}, u32[]{:S(2)}) copy-start(bf16[24,1,128,128]{3,2,1,0:T(8,128)(2,1)} %param.17) | copy-start | bytes 2359300
  68.9 94.7 %copy-start.4 = (bf16[8,3,384]{2,1,0:T(4,128)(2,1)S(1)}, bf16[8,3,384]{2,1,0:T(4,128)(2,1)}, u32[]{:S(2)}) copy-start(bf16[8,3,384]{2,1,0:T(4,128)(2,1)} %copy-done.3) | copy-start | bytes 55300
  86.2 33.6 %all-to-all-start.1 = ((f32[32,1,1152]{2,1,0:T(1,128)}), f32[32,1,1152]{2,1,0:T(1,128)S(1)}, u32[]{:S(2)}, u32[]{:S(2)}) async-start(f32[32,1,1152]{2,1,0:T(1,128)} %reshape.206), calls=%async_computation.1 | async-start | bytes 294912 | tf_op jit(solution)/shard_map/all_to_all | solution.py:33
  91.0 210.7 %all-gather.4.cloned.1.call-start = ((), (), s32[]{:S(2)}) async-start(), calls=%async_computation.5 | async-start | bytes 9732096 | tf_op jit(solution)/shard_map/all_gather | solution.py:60
Sparse Core Ops, SparseCore 0:
  163.7 137.9 all-gather.3
where the time goes:
time: 358 us; the launch traced here: 357 us
  blocking collectives  137 us (38%)
  waiting for transfers between devices  110 us (31%)
  starting transfers between devices  56.3 us (16%)
  other arithmetic  19.4 us (5%)
  local copies, waits for them, and re-layouts  15.8 us (4%)
  between operations  13.7 us (4%)
  matrix products  5.05 us (1%)
    all_gather x1, waiting for transfers between devices, side_by_side(): result = lax.all_gather(both, axis, axis=dim, tiled=True)  61.3 us
    all_to_all x2, blocking collectives, summed_on_arrival(): lax.all_to_all(tiles, axis, split_axis=0, concat_axis=0, tiled=True)  56 us
    all_to_all x2, waiting for transfers between devices, summed_on_arrival(): lax.all_to_all(tiles, axis, split_axis=0, concat_axis=0, tiled=True)  45.3 us
    all_to_all x1, starting transfers between devices, sent_to_all(): return lax.all_to_all(copies, axis, split_axis=0, concat_axis=0, tiled=True)  44.7 us
    all_gather x1, blocking collectives, in_one_piece_2(): lax.all_gather(both, axis, axis=dim, tiled=True)  42.9 us
    all_gather x1, blocking collectives, local(): lax.all_gather(queries, 'seq', axis=1, tiled=True)  38.6 us
    all_to_all x2, starting transfers between devices, summed_on_arrival(): lax.all_to_all(tiles, axis, split_axis=0, concat_axis=0, tiled=True)  11.5 us
    unnamed x19, local copies, waits for them, and re-layouts  10.6 us
  transfers between devices with their start and end apart: 4, of which 4 were waited for; matrix products, arithmetic and copies ran while one was open for 3% of the time, Pallas kernels for 0%

commit v1 on v0

--- a/solution.py
+++ b/solution.py
@@ -95,7 +95,7 @@
     new_keys = (key_sum * inverse_rms).astype(jnp.bfloat16)
     new_values = (value_sum * inverse_rms).astype(jnp.bfloat16)
     queries, new_keys, new_values = (
-        lax.all_gather(queries, "seq", axis=1, tiled=True),
+        jnp.concatenate(lax.all_gather(queries, "seq"), axis=1),
         *in_one_piece_2((new_keys, new_values), "seq", 1, 0),
     )
     grouped = queries.reshape(batch_size, kv_local, group_size, head_size)

time: 358 us -> 358 us (level)
    unnamed x19 -> x22, local copies, waits for them, and re-layouts: 10.6 us -> 10.3 us
  transfers between devices with their start and end apart: 4 -> 4, of which waited for: 4 -> 4; matrix products, arithmetic and copies ran while one was open for 3% -> 2% of each run, Pallas kernels for 0% -> 0%
where the time goes in v1:
time: 358 us
  blocking collectives  136 us (38%)
  waiting for transfers between devices  112 us (31%)
  starting transfers between devices  56.3 us (16%)
  other arithmetic  19.4 us (5%)
  local copies, waits for them, and re-layouts  15.6 us (4%)
  between operations  13.7 us (4%)
  matrix products  4.36 us (1%)
    all_gather x1, waiting for transfers between devices, side_by_side(): result = lax.all_gather(both, axis, axis=dim, tiled=True)  63.6 us
    all_to_all x2, blocking collectives, summed_on_arrival(): lax.all_to_all(tiles, axis, split_axis=0, concat_axis=0, tiled=True)  55.8 us
    all_to_all x2, waiting for transfers between devices, summed_on_arrival(): lax.all_to_all(tiles, axis, split_axis=0, concat_axis=0, tiled=True)  45.3 us
    all_to_all x1, starting transfers between devices, sent_to_all(): return lax.all_to_all(copies, axis, split_axis=0, concat_axis=0, tiled=True)  44.7 us
    all_gather x1, blocking collectives, in_one_piece_2(): lax.all_gather(both, axis, axis=dim, tiled=True)  41.9 us
    all_gather x1, blocking collectives, local(): lax.all_gather(queries, 'seq')  38.6 us
    all_to_all x2, starting transfers between devices, summed_on_arrival(): lax.all_to_all(tiles, axis, split_axis=0, concat_axis=0, tiled=True)  11.5 us
    unnamed x22, local copies, waits for them, and re-layouts  10.3 us
  transfers between devices with their start and end apart: 4, of which 4 were waited for; matrix products, arithmetic and copies ran while one was open for 2% of the time, Pallas kernels for 0%

profile of v1, /device:TPU:33, one launch (start us, length us, event | category | flops | bytes accessed | tf_op | source)
XLA Modules:
  0.0 357.7 jit_solution(17813467417402396910)
XLA Ops:
  6.6 1.4 broadcast_in_dim.49
  8.0 44.7 %all-to-all-start = ((bf16[8,3,384]{2,1,0:T(4,128)(2,1)}), bf16[8,3,384]{2,1,0:T(4,128)(2,1)S(1)}, u32[]{:S(2)}, u32[]{:S(2)}) async-start(bf16[8,3,384]{2,1,0:T(4,128)(2,1)} %broadcast_in_dim.49), calls=%async_computation | async-start | bytes 49152 | tf_op jit(solution)/shard_map/all_to_all | solution.py:19
  52.7 1.7 copy.65
  54.4 3.0 all-to-all-done
  57.4 0.8 multiply_reduce_fusion
  58.9 6.8 %all-to-all-start.2 = ((f32[32,24,1]{1,2,0:T(1,128)}), f32[32,24,1]{1,2,0:T(1,128)S(1)}, u32[]{:S(2)}, u32[]{:S(2)}) async-start(f32[32,24,1]{1,2,0:T(1,128)} %transpose.24), calls=%async_computation.2 | async-start | bytes 32768 | tf_op jit(solution)/shard_map/all_to_all | solution.py:33
  66.3 1.6 convolution_bitcast_fusion
  67.9 1.0 reshape.239
  68.9 17.3 %all-to-all-done.2 = f32[32,24,1]{1,2,0:T(1,128)S(1)} async-done(((f32[32,24,1]{1,2,0:T(1,128)}), f32[32,24,1]{1,2,0:T(1,128)S(1)}, u32[]{:S(2)}, u32[]{:S(2)}) %all-to-all-start.2) | async-done | bytes 3104 | tf_op jit(solution)/shard_map/all_to_all | solution.py:33
  86.2 4.8 %all-to-all-start.1 = ((f32[32,1,1152]{2,1,0:T(1,128)}), f32[32,1,1152]{2,1,0:T(1,128)S(1)}, u32[]{:S(2)}, u32[]{:S(2)}) async-start(f32[32,1,1152]{2,1,0:T(1,128)} %reshape.239), calls=%async_computation.1 | async-start | bytes 294912 | tf_op jit(solution)/shard_map/all_to_all | solution.py:33
  91.1 0.7 broadcast_compare_fusion
  91.9 27.9 %all-to-all-done.1 = f32[32,1,1152]{2,1,0:T(1,128)S(1)} async-done(((f32[32,1,1152]{2,1,0:T(1,128)}), f32[32,1,1152]{2,1,0:T(1,128)S(1)}, u32[]{:S(2)}, u32[]{:S(2)}) %all-to-all-start.1) | async-done | bytes 147488 | tf_op jit(solution)/shard_map/all_to_all | solution.py:33
  120.3 1.0 reduce.10
  121.7 38.6 %all_gather.10 = bf16[32,24,48]{2,1,0:T(8,128)(2,1)S(1)} all-gather(bf16[1,24,48]{2,1,0:T(8,128)(2,1)S(1)} %fusion.10), channel_id=1, replica_groups=mesh['parts'=2,'seq'=32,'head'=8] {'seq'}, dimensions={0}, use_global_device_ids=true | all-gather | bytes 76032 | tf_op jit(solution)/shard_map/all_gather | solution.py:98
  161.3 1.5 convolution_bitcast_fusion.1
  163.6 0.9 copy.71
  165.2 30.1 %all_to_all.25 = f32[32,1,192]{2,1,0:T(1,128)S(1)} all-to-all(f32[32,1,192]{2,1,0:T(1,128)S(1)} %reshape.241), channel_id=1, replica_groups=mesh['parts'=2,'seq'=32,'head'=8] {'seq'}, dimensions={0} | all-to-all | bytes 49152 | tf_op jit(solution)/shard_map/all_to_all | solution.py:33
  196.3 41.9 %all-gather = bf16[32,4,48]{2,1,0:T(4,128)(2,1)S(1)} all-gather(bf16[1,4,48]{2,1,0:T(4,128)(2,1)S(1)} %maximum_bitcast_fusion), channel_id=1, replica_groups=mesh['parts'=2,'seq'=32,'head'=8] {'seq'}, dimensions={0}, use_global_device_ids=true | all-gather | bytes 12672 | tf_op jit(solution)/shard_map/all_gather | solution.py:52
  238.6 63.6 %all-gather.3.cloned.1.call-done = f32[32,24,1,12,130]{4,1,3,2,0:T(8,128)} async-done(((f32[1,24,1,12,130]{4,1,3,2,0:T(8,128)}), f32[32,24,1,12,130]{4,1,3,2,0:T(8,128)}) %all-gather.3.cloned.1.call-update) | async-done | bytes 4792336 | tf_op jit(solution)/shard_map/all_gather | solution.py:60
  302.2 9.1 %fusion.19 = (f32[32,24,1,12,1]{4,1,3,2,0:T(8,128)}, f32[24,12]{0,1:T(8,128)S(1)}, f32[32,24,1,12,1]{4,1,3,2,0:T(8,128)}) fusion(f32[32,24,1,12,130]{4,1,3,2,0:T(8,128)} %all-gather.3.cloned.1.call-done), kind=kLoop, calls=%fused_computation.46 | loop fusion | flops 8928 | bytes 148608 | tf_op jit(solution)/shard_map/split | solution.py:61
  311.3 3.5 copy.87
  314.8 3.5 copy.86
  318.8 5.1 %fusion = f32[24,12,128]{2,0,1:T(8,128)S(1)} fusion(f32[32,24,1,12,130]{4,1,3,2,0:T(8,128)} %all-gather.3.cloned.1.call-done, f32[32,24,12]{1,2,0:T(8,128)S(1)} %copy.73), kind=kLoop, calls=%fused_computation.1 | loop fusion | flops 2322432 | bytes 4902912 | tf_op jit(solution)/shard_map/reduce_sum | solution.py:71
  324.5 25.7 %all_to_all.26 = f32[8,3,384]{2,1,0:T(4,128)S(1)} all-to-all(f32[8,3,384]{2,1,0:T(4,128)S(1)} %copy.79), channel_id=1, replica_groups=mesh['parts'=2,'seq'=32,'head'=8] {'head'}, dimensions={0} | all-to-all | bytes 73728 | tf_op jit(solution)/shard_map/all_to_all | solution.py:33
  (59 shorter events, 7.7 us)
Async XLA Ops:
  6.5 317.6 %copy-start = (bf16[1536,384]{1,0:T(8,128)(2,1)S(1)}, bf16[1536,384]{1,0:T(8,128)(2,1)}, u32[]{:S(2)}) copy-start(bf16[1536,384]{1,0:T(8,128)(2,1)} %param.14) | copy-start | bytes 3538948
  6.6 153.9 %copy-start.1 = (bf16[24,1,128,128]{3,2,1,0:T(8,128)(2,1)S(1)}, bf16[24,1,128,128]{3,2,1,0:T(8,128)(2,1)}, u32[]{:S(2)}) copy-start(bf16[24,1,128,128]{3,2,1,0:T(8,128)(2,1)} %param.16) | copy-start | bytes 2359300
  8.0 49.4 %all-to-all-start = ((bf16[8,3,384]{2,1,0:T(4,128)(2,1)}), bf16[8,3,384]{2,1,0:T(4,128)(2,1)S(1)}, u32[]{:S(2)}, u32[]{:S(2)}) async-start(bf16[8,3,384]{2,1,0:T(4,128)(2,1)} %broadcast_in_dim.49), calls=%async_computation | async-start | bytes 49152 | tf_op jit(solution)/shard_map/all_to_all | solution.py:19
  57.4 8.9 %copy-start.2 = (bf16[8,3,384]{2,1,0:T(4,128)(2,1)}, bf16[8,3,384]{2,1,0:T(4,128)(2,1)S(1)}, u32[]{:S(2)}) copy-start(bf16[8,3,384]{2,1,0:T(4,128)(2,1)S(1)} %all-to-all-done) | copy-start | bytes 55300
  58.9 27.3 %all-to-all-start.2 = ((f32[32,24,1]{1,2,0:T(1,128)}), f32[32,24,1]{1,2,0:T(1,128)S(1)}, u32[]{:S(2)}, u32[]{:S(2)}) async-start(f32[32,24,1]{1,2,0:T(1,128)} %transpose.24), calls=%async_computation.2 | async-start | bytes 32768 | tf_op jit(solution)/shard_map/all_to_all | solution.py:33
  67.8 96.7 %copy-start.3 = (bf16[8,3,384]{2,1,0:T(4,128)(2,1)S(1)}, bf16[8,3,384]{2,1,0:T(4,128)(2,1)}, u32[]{:S(2)}) copy-start(bf16[8,3,384]{2,1,0:T(4,128)(2,1)} %copy-done.2) | copy-start | bytes 55300
  67.8 96.8 %copy-start.4 = (bf16[384,128]{1,0:T(8,128)(2,1)S(1)}, bf16[384,128]{1,0:T(8,128)(2,1)}, u32[]{:S(2)}) copy-start(bf16[384,128]{1,0:T(8,128)(2,1)} %param.13) | copy-start | bytes 294916
  67.8 96.8 %copy-start.6 = (f32[384]{0:T(512)S(1)}, f32[384]{0:T(512)}, u32[]{:S(2)}) copy-start(f32[384]{0:T(512)} %param.10) | copy-start | bytes 4612
  67.9 96.9 %copy-start.5 = (bf16[384,128]{1,0:T(8,128)(2,1)S(1)}, bf16[384,128]{1,0:T(8,128)(2,1)}, u32[]{:S(2)}) copy-start(bf16[384,128]{1,0:T(8,128)(2,1)} %param.12) | copy-start | bytes 294916
  86.2 33.6 %all-to-all-start.1 = ((f32[32,1,1152]{2,1,0:T(1,128)}), f32[32,1,1152]{2,1,0:T(1,128)S(1)}, u32[]{:S(2)}, u32[]{:S(2)}) async-start(f32[32,1,1152]{2,1,0:T(1,128)} %reshape.239), calls=%async_computation.1 | async-start | bytes 294912 | tf_op jit(solution)/shard_map/all_to_all | solution.py:33
  91.0 211.2 %all-gather.3.cloned.1.call-start = ((), (), s32[]{:S(2)}) async-start(), calls=%async_computation.5 | async-start | bytes 9732096 | tf_op jit(solution)/shard_map/all_gather | solution.py:60
Sparse Core Ops, SparseCore 0:
  164.7 137.4 all-gather.2
